TPU v7x, 32 devices: a whole 2x2x4 slice. The times are simulated.
32 devices in a mesh: seq: 16 (over z, y, x), head: 2 (over core).
Axes of the slice: x: 2, y: 2, z: 4, core: 2. Of those that a mesh axis runs over, the one named last changes fastest.
Arguments:
- queries: bfloat16 [2048, 2048], P('seq', 'head'), may hold values from -6 to 6
- key_vectors: bfloat16 [2, 2048, 2048], P(None, 'seq', 'head'), may hold values from -6 to 6
- values: bfloat16 [2, 2048, 2048], P(None, 'seq', 'head'), may hold values from -6 to 6
- strengths: float32 [2, 16, 2048], P(None, 'head', 'seq'), may hold values from 0.05 to 1.95
- out_weight: bfloat16 [2048, 4096], P('head', 'seq'), may hold values from -0.1875 to 0.1875
Outputs:
- mixed: bfloat16 [2048, 4096], P('seq', 'head')
All inputs are finite; a program needn't handle non-finite values.
Results may differ from a plain program's by a relative error of at most 0.014.
Values may be sent and summed in bfloat16 or wider, within the bound.
No kernel may reach another device: no remote copies, remote signals or barrier semaphores. Data moves between devices by JAX's collectives and lax.ppermute only.
A program may use at most 64 MiB of HBM per device.

v0:
```python
import jax
import jax.numpy as jnp
from jax import lax
from jax.sharding import PartitionSpec as P

BLOCK = 64
HIGHEST_PRECISION = lax.Precision.HIGHEST


def carried_in(value, axis, join, neutral):
    count, mine = (lax.axis_size(axis), lax.axis_index(axis))
    pieces = jax.tree.map(lambda part: lax.all_gather(part, axis), value)
    total = jax.tree.map(
        lambda part, zero: jnp.full_like(part, 0) + jnp.asarray(zero, part.dtype), value, neutral
    )

    def hop(position, total):
        longer = join(total, jax.tree.map(lambda part: part[position], pieces))
        return jax.tree.map(lambda new, old: jnp.where(position < mine, new, old), longer, total)

    return lax.fori_loop(0, count - 1, hop, total)


def unit_rows(matrix):
    return matrix * lax.rsqrt(jnp.sum(matrix * matrix, axis=-1, keepdims=True) + 1e-06)


def block_inputs(inputs, first_row):
    queries, key_vectors, values, strengths = inputs
    head_count = strengths.shape[1]
    head_width = queries.shape[1] // head_count
    query_part = (
        lax.dynamic_slice_in_dim(queries, first_row, BLOCK, 0)
        .astype(jnp.float32)
        .reshape(BLOCK, head_count, head_width)
    )
    key_part = (
        lax.dynamic_slice_in_dim(key_vectors, first_row, BLOCK, 1)
        .astype(jnp.float32)
        .reshape(2, BLOCK, head_count, head_width)
    )
    value_part = (
        lax.dynamic_slice_in_dim(values, first_row, BLOCK, 1)
        .astype(jnp.float32)
        .reshape(2, BLOCK, head_count, head_width)
    )
    beta_part = lax.dynamic_slice_in_dim(strengths, first_row, BLOCK, 2)
    query_heads = jnp.transpose(unit_rows(query_part), (1, 0, 2))
    key_heads = jnp.transpose(unit_rows(key_part), (2, 1, 0, 3)).reshape(
        head_count, 2 * BLOCK, head_width
    )
    value_heads = jnp.transpose(value_part, (2, 1, 0, 3)).reshape(head_count, 2 * BLOCK, head_width)
    beta_heads = jnp.transpose(beta_part, (1, 2, 0)).reshape(head_count, 2 * BLOCK)
    return (query_heads, key_heads, value_heads, beta_heads)


def solve_block(key_heads, right_side, beta_heads):
    key_gram = jnp.einsum("hik,hjk->hij", key_heads, key_heads, precision=HIGHEST_PRECISION)
    system = jnp.tril(key_gram, -1) * beta_heads[:, :, None] + jnp.eye(2 * BLOCK, dtype=jnp.float32)
    return jax.scipy.linalg.solve_triangular(
        system, beta_heads[:, :, None] * right_side, lower=True, unit_diagonal=True
    )


def reach_table():
    row_ids = lax.broadcasted_iota(jnp.int32, (BLOCK, 2 * BLOCK), 0)
    col_ids = lax.broadcasted_iota(jnp.int32, (BLOCK, 2 * BLOCK), 1)
    return (col_ids <= 2 * row_ids + 1).astype(jnp.float32)


def compose(earlier, later):
    product = jnp.einsum("hjk,hkl->hjl", earlier[0], later[0], precision=HIGHEST_PRECISION)
    state = jnp.einsum("hjk,hkl->hjl", earlier[1], later[0], precision=HIGHEST_PRECISION) + later[1]
    return (product, state)


def incoming_state(product, local_state, identity_stack, zero_state):
    prefix = carried_in((product, local_state), "seq", compose, (identity_stack, zero_state))
    return prefix[1]


def per_device(queries, key_vectors, values, strengths, out_weight):
    head_count = strengths.shape[1]
    tok_rows = queries.shape[0]
    head_width = queries.shape[1] // head_count
    inputs = (queries, key_vectors, values, strengths)
    first_rows = jnp.arange(tok_rows // BLOCK, dtype=jnp.int32) * BLOCK
    identity_stack = jnp.broadcast_to(
        jnp.eye(head_width, dtype=jnp.float32), (head_count, head_width, head_width)
    )
    zero_state = jnp.zeros((head_count, head_width, head_width), jnp.float32)
    reach_mask = reach_table()

    def ahead_step(carried, first_row):
        local_state, product = carried
        query_heads, key_heads, value_heads, beta_heads = block_inputs(inputs, first_row)
        solved = solve_block(
            key_heads, jnp.concatenate([key_heads, value_heads], axis=2), beta_heads
        )
        key_weights = solved[:, :, :head_width]
        value_weights = solved[:, :, head_width:]
        scores = (
            jnp.einsum("htk,hik->hti", query_heads, key_heads, precision=HIGHEST_PRECISION)
            * reach_mask
        )
        updates = value_weights - jnp.einsum(
            "hik,hvk->hiv", key_weights, local_state, precision=HIGHEST_PRECISION
        )
        out_local = jnp.einsum(
            "hvk,htk->htv", local_state, query_heads, precision=HIGHEST_PRECISION
        ) + jnp.einsum("hti,hiv->htv", scores, updates, precision=HIGHEST_PRECISION)
        reduced = query_heads - jnp.einsum(
            "hti,hik->htk", scores, key_weights, precision=HIGHEST_PRECISION
        )
        lifted = jnp.einsum("htk,hjk->htj", reduced, product, precision=HIGHEST_PRECISION)
        shrink = identity_stack - jnp.einsum(
            "hik,hil->hkl", key_weights, key_heads, precision=HIGHEST_PRECISION
        )
        local_state = local_state + jnp.einsum(
            "hiv,hik->hvk", updates, key_heads, precision=HIGHEST_PRECISION
        )
        product = jnp.einsum("hjk,hkl->hjl", product, shrink, precision=HIGHEST_PRECISION)
        return ((local_state, product), (out_local, lifted))

    (local_state, product), (out_local, lifted) = lax.scan(
        ahead_step, (zero_state, identity_stack), first_rows
    )
    state_in = incoming_state(product, local_state, identity_stack, zero_state)
    heads_out = out_local + jnp.einsum(
        "nhtk,hvk->nhtv", lifted, state_in, precision=HIGHEST_PRECISION
    )
    mixed_heads = (
        jnp.transpose(heads_out, (0, 2, 1, 3))
        .reshape(tok_rows, head_count * head_width)
        .astype(jnp.bfloat16)
    )
    partial_sums = jnp.dot(
        mixed_heads,
        lax.all_gather(out_weight, "seq", axis=1, tiled=True),
        preferred_element_type=jnp.float32,
    )
    return lax.psum_scatter(
        partial_sums.astype(jnp.bfloat16), "head", scatter_dimension=1, tiled=True
    )


def solution(mesh):
    return jax.shard_map(
        per_device,
        mesh=mesh,
        in_specs=(
            P("seq", "head"),
            P(None, "seq", "head"),
            P(None, "seq", "head"),
            P(None, "head", "seq"),
            P("head", "seq"),
        ),
        out_specs=P("seq", "head"),
        check_vma=False,
    )
```

profile of v0, /device:TPU:0, one launch (start us, length us, event | category | flops | bytes accessed | tf_op | source)
XLA Modules:
  0.0 591.6 jit_solution(15922539583316434189)
XLA Ops:
  6.7 200.9 %while.31 = (s32[]{:T(128)}, f32[8,128,128]{2,1,0:T(8,128)S(1)}, f32[8,128,128]{1,2,0:T(8,128)S(1)}, f32[2,8,64,128]{3,2,0,1:T(8,128)}, f32[2,8,64,128]{3,2,0,1:...) while((s32[]{:T(128)}, f32[8,128,128]{2,1,0:T(8,128)S(1)}, ...), condition=%wide.region_3.4_spmd.clone, body=%wide.region_0.3_spmd.clone.sunk | while | flops 1915912320 | bytes 28152272 | solution.py:125
  9.3 1.2 dynamic-slice_convert_fusion.3
  12.5 1.2 fusion.128
  13.8 79.2 %custom-call.10 = f32[8,1,128,128]{2,3,1,0:T(8,128)} custom-call(f32[8,1,128,128]{3,2,1,0:T(8,128)S(1)} %fusion.128), custom_call_target="InvertDiagBlocksLowerTriangular" | custom-call | tf_op jit(solution)/shard_map/while/body/eval_jaxpr/jit(_solve_triangular)/vmap()/triangular_solve | solution.py:60
  93.6 2.3 fusion.129
  95.9 1.2 convolution_subtract_fusion.6
  97.1 1.0 convert_bitcast_fusion.3
  98.4 1.1 convolution_multiply_fusion.2
  99.5 1.1 fusion.130
  100.7 1.3 fusion.132
  102.0 1.0 convolution_subtract_fusion.7
  103.6 1.3 fusion.133
  104.9 1.0 convolution_bitcast_fusion.5
  106.0 1.1 convolution_add_fusion.3
  109.6 1.2 dynamic-slice_convert_fusion.3
  112.9 1.2 fusion.128
  114.1 79.2 %custom-call.10 = f32[8,1,128,128]{2,3,1,0:T(8,128)} custom-call(f32[8,1,128,128]{3,2,1,0:T(8,128)S(1)} %fusion.128), custom_call_target="InvertDiagBlocksLowerTriangular" | custom-call | tf_op jit(solution)/shard_map/while/body/eval_jaxpr/jit(_solve_triangular)/vmap()/triangular_solve | solution.py:60
  193.9 2.3 fusion.129
  196.2 1.2 convolution_subtract_fusion.6
  197.4 1.0 convert_bitcast_fusion.3
  198.7 1.1 convolution_multiply_fusion.2
  199.8 1.1 fusion.130
  201.0 1.3 fusion.132
  202.3 1.0 convolution_subtract_fusion.7
  204.0 1.3 fusion.133
  205.3 1.0 convolution_bitcast_fusion.5
  206.3 1.1 convolution_add_fusion.3
  207.6 1.1 copy.94
  210.3 113.6 %all-gather.8.cloned.1.call-done = f32[128,128,128]{2,1,0:T(8,128)} async-done(((f32[8,128,128]{2,1,0:T(8,128)}), f32[128,128,128]{2,1,0:T(8,128)}) %all-gather.8.cloned.1.call-update) | async-done | bytes 8388624 | tf_op jit(solution)/shard_map/all_gather | solution.py:12
  323.9 113.3 %all-gather.10.cloned.1.call-done = f32[128,128,128]{2,1,0:T(8,128)} async-done(((f32[8,128,128]{2,1,0:T(8,128)}), f32[128,128,128]{2,1,0:T(8,128)}) %all-gather.10.cloned.1.call-update) | async-done | bytes 8388624 | tf_op jit(solution)/shard_map/all_gather | solution.py:12
  437.2 51.5 %while.32 = (s32[]{:T(128)}, f32[8,128,128]{1,2,0:T(8,128)S(1)}, s32[]{:T(128)}, f32[16,8,128,128]{3,2,1,0:T(8,128)}, f32[16,8,128,128]{3,2,1,0:T(8,128)}, /*index=5*/s32[]{:T(128)}, s32[]{:T(128)}) while((s32[]{:T(128)}, f32[8,128,128]{1,2,0:T(8,128)S(1)}, s32[]{:T(128)}, f32[16,8,128,128]{3,2,1,0:T(8,128)}, ...), condition=%wide.region_5.6_spmd.clone, body=%wide.region_4.5_spmd.clone.sunk | while | flops 201850880 | bytes 5769315 | solution.py:21
  437.2 1.2 constant_dynamic-slice_fusion.5
  438.6 2.1 fusion.136
  440.7 1.1 constant_dynamic-slice_fusion.5
  442.0 2.1 fusion.136
  444.1 1.1 constant_dynamic-slice_fusion.5
  445.4 2.1 fusion.136
  447.6 1.1 constant_dynamic-slice_fusion.5
  448.9 2.1 fusion.136
  451.0 1.1 constant_dynamic-slice_fusion.5
  452.3 2.1 fusion.136
  454.4 1.1 constant_dynamic-slice_fusion.5
  455.8 2.1 fusion.136
  457.8 1.1 constant_dynamic-slice_fusion.5
  459.2 2.1 fusion.136
  461.3 1.1 constant_dynamic-slice_fusion.5
  462.6 2.1 fusion.136
  464.7 1.1 constant_dynamic-slice_fusion.5
  466.0 2.1 fusion.136
  468.1 1.1 constant_dynamic-slice_fusion.5
  469.4 2.1 fusion.136
  471.6 1.1 constant_dynamic-slice_fusion.5
  472.9 2.1 fusion.136
  475.0 1.1 constant_dynamic-slice_fusion.5
  476.3 2.1 fusion.136
  478.4 1.1 constant_dynamic-slice_fusion.5
  479.7 2.1 fusion.136
  481.8 1.1 constant_dynamic-slice_fusion.5
  483.2 2.1 fusion.136
  485.3 1.1 constant_dynamic-slice_fusion.5
  486.6 2.1 fusion.136
  489.5 83.1 %all-gather.6.cloned.1.call-done = bf16[1024,4096]{1,0:T(8,128)(2,1)} async-done(((bf16[1024,256]{1,0:T(8,128)(2,1)}), bf16[1024,4096]{1,0:T(8,128)(2,1)}) %all-gather.6.cloned.1.call-update) | async-done | bytes 8388624 | tf_op jit(solution)/shard_map/all_gather | solution.py:139
  572.6 5.7 convolution_convert_fusion
  578.3 6.7 %reduce-scatter.2.cloned.1.call-done = bf16[128,2048]{1,0:T(8,128)(2,1)} async-done(((bf16[128,4096]{1,0:T(8,128)(2,1)}), bf16[128,2048]{1,0:T(8,128)(2,1)}) %reduce-scatter.2.cloned.1.call-update) | async-done | bytes 524304 | tf_op jit(solution)/shard_map/reduce_scatter | solution.py:142
  (99 shorter events, 14.2 us)
Async XLA Ops:
  6.5 317.4 %all-gather.8.cloned.1.call-start = ((), (), s32[]{:S(2)}) async-start(), calls=%async_computation.3 | async-start | bytes 8912896 | tf_op jit(solution)/shard_map/all_gather | solution.py:12
  207.6 1.1 copy-start
  208.7 228.5 %all-gather.10.cloned.1.call-start = ((), (), s32[]{:S(2)}) async-start(), calls=%async_computation.4 | async-start | bytes 8912896 | tf_op jit(solution)/shard_map/all_gather | solution.py:12
  209.5 363.1 %all-gather.6.cloned.1.call-start = ((), (), s32[]{:S(2)}) async-start(), calls=%async_computation.1 | async-start | bytes 8912896 | tf_op jit(solution)/shard_map/all_gather | solution.py:139
  210.2 374.8 %reduce-scatter.2.cloned.1.call-start = ((), (), s32[]{:S(2)}) async-start(), calls=%async_computation.2 | async-start | bytes 1572864 | tf_op jit(solution)/shard_map/reduce_scatter | solution.py:142
  437.2 51.5 %copy-start.1 = (f32[2,8,64,128]{3,2,0,1:T(8,128)S(1)}, f32[2,8,64,128]{3,2,0,1:T(8,128)}, u32[]{:S(2)}) copy-start(f32[2,8,64,128]{3,2,0,1:T(8,128)} %get-tuple-element.164) | copy-start | bytes 1572868
  437.2 51.5 %copy-start.2 = (f32[2,8,64,128]{3,2,0,1:T(8,128)S(1)}, f32[2,8,64,128]{3,2,0,1:T(8,128)}, u32[]{:S(2)}) copy-start(f32[2,8,64,128]{3,2,0,1:T(8,128)} %get-tuple-element.168) | copy-start | bytes 1572868
Sparse Core Ops, SparseCore 0:
  208.8 115.0 all-gather.7
  326.7 110.4 all-gather.9
  439.9 132.6 all-gather.5
  578.4 6.5 reduce-scatter.1
where the time goes:
time: 593 us; the launch traced here: 592 us
  waiting for transfers between devices  318 us (54%)
  other arithmetic  164 us (28%)
  matrix products  64 us (11%)
  local copies, waits for them, and re-layouts  26.7 us (5%)
  between operations  13.3 us (2%)
    all_gather x2, waiting for transfers between devices, carried_in(): pieces = jax.tree.map(lambda part: lax.all_gather(part, axis), value)  227 us
    another operation x8, other arithmetic, solve_block(): jax.scipy.linalg.solve_triangular(system, beta_heads[:, :, None] * right_...  159 us
    all_gather x1, waiting for transfers between devices, per_device(): lax.all_gather(out_weight, 'seq', axis=1, tiled=True)  83.1 us
    dot_general x15, matrix products, compose(): jnp.einsum('hjk,hkl->hjl', earlier[1], later[0], precision=HIGHEST_PRECIS...  31 us
    dynamic_slice x30, local copies, waits for them, and re-layouts, hop(): longer = join(total, jax.tree.map(lambda part: part[position], pieces))  19.3 us
  transfers between devices with their start and end apart: 4, of which 4 were waited for; matrix products, arithmetic and copies ran while one was open for 9% of the time, Pallas kernels for 0%

commit v1 on v0

--- a/solution.py
+++ b/solution.py
@@ -136,7 +136,7 @@
     )
     partial_sums = jnp.dot(
         mixed_heads,
-        lax.all_gather(out_weight, "seq", axis=1, tiled=True),
+        jnp.concatenate(lax.all_gather(out_weight, "seq"), axis=1),
         preferred_element_type=jnp.float32,
     )
     return lax.psum_scatter(

time: 593 us -> 585 us (0.987)
  waiting for transfers between devices: 318 us -> 296 us
  local copies, waits for them, and re-layouts: 26.7 us -> 39 us
    all_gather x1, waiting for transfers between devices: 83.1 us -> 60.9 us  [per_device(): lax.all_gather(out_weight, 'seq')]
    reshape x0 -> x1, local copies, waits for them, and re-layouts: none -> 12.3 us  [per_device(): jnp.concatenate(lax.all_gather(out_weight, 'seq'), axis=1)]
where the time goes in v1:
time: 585 us; the launch traced here: 583 us
  waiting for transfers between devices  296 us (51%)
  other arithmetic  164 us (28%)
  matrix products  65.5 us (11%)
  local copies, waits for them, and re-layouts  39 us (7%)
  between operations  13.3 us (2%)
    all_gather x2, waiting for transfers between devices, carried_in(): pieces = jax.tree.map(lambda part: lax.all_gather(part, axis), value)  227 us
    another operation x8, other arithmetic, solve_block(): jax.scipy.linalg.solve_triangular(system, beta_heads[:, :, None] * right_...  159 us
    all_gather x1, waiting for transfers between devices, per_device(): lax.all_gather(out_weight, 'seq')  60.9 us
    dot_general x15, matrix products, compose(): jnp.einsum('hjk,hkl->hjl', earlier[1], later[0], precision=HIGHEST_PRECIS...  30.9 us
    dynamic_slice x30, local copies, waits for them, and re-layouts, hop(): longer = join(total, jax.tree.map(lambda part: part[position], pieces))  19.3 us
    reshape x1, local copies, waits for them, and re-layouts, per_device(): jnp.concatenate(lax.all_gather(out_weight, 'seq'), axis=1)  12.3 us
  transfers between devices with their start and end apart: 4, of which 4 were waited for; matrix products, arithmetic and copies ran while one was open for 9% of the time, Pallas kernels for 0%

profile of v1, /device:TPU:0, one launch (start us, length us, event | category | flops | bytes accessed | tf_op | source)
XLA Modules:
  0.0 583.2 jit_solution(10554722482029041547)
XLA Ops:
  6.7 200.9 %while.31 = (s32[]{:T(128)}, f32[8,128,128]{2,1,0:T(8,128)S(1)}, f32[8,128,128]{1,2,0:T(8,128)S(1)}, f32[2,8,64,128]{3,2,0,1:T(8,128)}, f32[2,8,64,128]{3,2,0,1:...) while((s32[]{:T(128)}, f32[8,128,128]{2,1,0:T(8,128)S(1)}, ...), condition=%wide.region_3.4_spmd.clone, body=%wide.region_0.3_spmd.clone.sunk | while | flops 1915912320 | bytes 28152272 | solution.py:125
  9.3 1.2 dynamic-slice_convert_fusion.3
  12.5 1.2 fusion.128
  13.8 79.2 %custom-call.10 = f32[8,1,128,128]{2,3,1,0:T(8,128)} custom-call(f32[8,1,128,128]{3,2,1,0:T(8,128)S(1)} %fusion.128), custom_call_target="InvertDiagBlocksLowerTriangular" | custom-call | tf_op jit(solution)/shard_map/while/body/eval_jaxpr/jit(_solve_triangular)/vmap()/triangular_solve | solution.py:60
  93.6 2.3 fusion.129
  95.9 1.2 convolution_subtract_fusion.6
  97.1 1.0 convert_bitcast_fusion.3
  98.4 1.1 convolution_multiply_fusion.2
  99.5 1.1 fusion.130
  100.7 1.3 fusion.132
  102.0 1.0 convolution_subtract_fusion.7
  103.6 1.3 fusion.133
  104.9 1.0 convolution_bitcast_fusion.5
  106.0 1.1 convolution_add_fusion.3
  109.6 1.2 dynamic-slice_convert_fusion.3
  112.9 1.2 fusion.128
  114.1 79.2 %custom-call.10 = f32[8,1,128,128]{2,3,1,0:T(8,128)} custom-call(f32[8,1,128,128]{3,2,1,0:T(8,128)S(1)} %fusion.128), custom_call_target="InvertDiagBlocksLowerTriangular" | custom-call | tf_op jit(solution)/shard_map/while/body/eval_jaxpr/jit(_solve_triangular)/vmap()/triangular_solve | solution.py:60
  193.9 2.3 fusion.129
  196.2 1.2 convolution_subtract_fusion.6
  198.7 1.1 convolution_multiply_fusion.2
  199.8 1.1 fusion.130
  201.0 1.3 fusion.132
  202.3 1.0 convolution_subtract_fusion.7
  204.0 1.3 fusion.133
  205.3 1.0 convolution_bitcast_fusion.5
  206.3 1.1 convolution_add_fusion.3
  207.6 1.1 copy.112
  210.3 113.6 %all-gather.7.cloned.1.call-done = f32[128,128,128]{2,1,0:T(8,128)} async-done(((f32[8,128,128]{2,1,0:T(8,128)}), f32[128,128,128]{2,1,0:T(8,128)}) %all-gather.7.cloned.1.call-update) | async-done | bytes 8388624 | tf_op jit(solution)/shard_map/all_gather | solution.py:12
  323.9 113.3 %all-gather.9.cloned.1.call-done = f32[128,128,128]{2,1,0:T(8,128)} async-done(((f32[8,128,128]{2,1,0:T(8,128)}), f32[128,128,128]{2,1,0:T(8,128)}) %all-gather.9.cloned.1.call-update) | async-done | bytes 8388624 | tf_op jit(solution)/shard_map/all_gather | solution.py:12
  437.2 51.5 %while.32 = (s32[]{:T(128)}, f32[8,128,128]{1,2,0:T(8,128)S(1)}, s32[]{:T(128)}, f32[16,8,128,128]{3,2,1,0:T(8,128)}, f32[16,8,128,128]{3,2,1,0:T(8,128)}, /*index=5*/s32[]{:T(128)}, s32[]{:T(128)}) while((s32[]{:T(128)}, f32[8,128,128]{1,2,0:T(8,128)S(1)}, s32[]{:T(128)}, f32[16,8,128,128]{3,2,1,0:T(8,128)}, ...), condition=%wide.region_5.6_spmd.clone, body=%wide.region_4.5_spmd.clone.sunk | while | flops 201850880 | bytes 5769315 | solution.py:21
  437.2 1.2 constant_dynamic-slice_fusion.5
  438.6 2.1 fusion.136
  440.7 1.1 constant_dynamic-slice_fusion.5
  442.0 2.1 fusion.136
  444.1 1.1 constant_dynamic-slice_fusion.5
  445.4 2.1 fusion.136
  447.6 1.1 constant_dynamic-slice_fusion.5
  448.9 2.1 fusion.136
  451.0 1.1 constant_dynamic-slice_fusion.5
  452.4 2.1 fusion.136
  454.4 1.1 constant_dynamic-slice_fusion.5
  455.8 2.1 fusion.136
  457.9 1.1 constant_dynamic-slice_fusion.5
  459.2 2.1 fusion.136
  461.3 1.1 constant_dynamic-slice_fusion.5
  462.6 2.1 fusion.136
  464.7 1.1 constant_dynamic-slice_fusion.5
  466.0 2.1 fusion.136
  468.1 1.1 constant_dynamic-slice_fusion.5
  469.5 2.1 fusion.136
  471.5 1.1 constant_dynamic-slice_fusion.5
  472.9 2.1 fusion.136
  475.0 1.1 constant_dynamic-slice_fusion.5
  476.3 2.1 fusion.136
  478.4 1.1 constant_dynamic-slice_fusion.5
  479.7 2.1 fusion.136
  481.8 1.1 constant_dynamic-slice_fusion.5
  483.2 2.1 fusion.136
  485.2 1.1 constant_dynamic-slice_fusion.5
  486.6 2.1 fusion.136
  489.5 60.9 %all-gather.11.cloned.1.call-done = bf16[16384,256]{1,0:T(8,128)(2,1)} async-done(((bf16[1024,256]{1,0:T(8,128)(2,1)}), bf16[16384,256]{1,0:T(8,128)(2,1)}) %all-gather.11.cloned.1.call-update) | async-done | bytes 8388624 | tf_op jit(solution)/shard_map/all_gather | solution.py:139
  550.4 12.3 %copy.119 = bf16[1024,16,256]{0,2,1:T(8,128)(2,1)} copy(bf16[1024,16,256]{2,0,1:T(8,128)(2,1)} %bitcast.212) | data formatting | bytes 16777216 | tf_op jit(solution)/shard_map/reshape | solution.py:139
  562.7 7.2 %convolution_convert_fusion = bf16[128,4096]{1,0:T(8,128)(2,1)} fusion(bf16[1024,4096]{0,1:T(8,128)(2,1)} %bitcast.210, bf16[16,8,8,128]{3,2,1,0:T(8,128)(2,1)S(1)} %bitcast.214), kind=kOutput, calls=%fused_computation.74 | convolution fusion | flops 1074266112 | bytes 9699328 | tf_op jit(solution)/shard_map/dot_general | solution.py:137
  570.0 6.7 %reduce-scatter.2.cloned.1.call-done = bf16[128,2048]{1,0:T(8,128)(2,1)} async-done(((bf16[128,4096]{1,0:T(8,128)(2,1)}), bf16[128,2048]{1,0:T(8,128)(2,1)}) %reduce-scatter.2.cloned.1.call-update) | async-done | bytes 524304 | tf_op jit(solution)/shard_map/reduce_scatter | solution.py:142
  (100 shorter events, 15.2 us)
Async XLA Ops:
  6.5 317.4 %all-gather.7.cloned.1.call-start = ((), (), s32[]{:S(2)}) async-start(), calls=%async_computation.2 | async-start | bytes 8912896 | tf_op jit(solution)/shard_map/all_gather | solution.py:12
  207.6 1.1 copy-start
  208.7 228.5 %all-gather.9.cloned.1.call-start = ((), (), s32[]{:S(2)}) async-start(), calls=%async_computation.3 | async-start | bytes 8912896 | tf_op jit(solution)/shard_map/all_gather | solution.py:12
  209.5 341.0 %all-gather.11.cloned.1.call-start = ((), (), s32[]{:S(2)}) async-start(), calls=%async_computation.4 | async-start | bytes 8912896 | tf_op jit(solution)/shard_map/all_gather | solution.py:139
  210.2 366.5 %reduce-scatter.2.cloned.1.call-start = ((), (), s32[]{:S(2)}) async-start(), calls=%async_computation.1 | async-start | bytes 1572864 | tf_op jit(solution)/shard_map/reduce_scatter | solution.py:142
  437.2 51.5 %copy-start.1 = (f32[2,8,64,128]{3,2,0,1:T(8,128)S(1)}, f32[2,8,64,128]{3,2,0,1:T(8,128)}, u32[]{:S(2)}) copy-start(f32[2,8,64,128]{3,2,0,1:T(8,128)} %get-tuple-element.164) | copy-start | bytes 1572868
  437.2 51.5 %copy-start.2 = (f32[2,8,64,128]{3,2,0,1:T(8,128)S(1)}, f32[2,8,64,128]{3,2,0,1:T(8,128)}, u32[]{:S(2)}) copy-start(f32[2,8,64,128]{3,2,0,1:T(8,128)} %get-tuple-element.168) | copy-start | bytes 1572868
Sparse Core Ops, SparseCore 0:
  208.8 115.0 all-gather.6
  326.7 110.4 all-gather.8
  439.9 110.4 all-gather.10
  570.1 6.5 reduce-scatter.1
